TPU v7x, 32 devices: a whole 2x2x4 slice. The times are simulated.
32 devices in a mesh: train: 4 (over z), serve: 8 (over y, x, core).
Axes of the slice: x: 2, y: 2, z: 4, core: 2. Of those that a mesh axis runs over, the one named last changes fastest.
Arguments:
- train_weights: bfloat16 [16, 7424, 2112], P(None, 'train', 'serve'), may hold values from -6 to 6
- row_offset: int32 [16, 5], replicated, may hold values from 0 to 7168, as said below
- block_group: int32 [16, 224, 1], P(None, 'train'), may hold values from 0 to 7; in each aligned block of 56 rows (0 to 55, 56 to 111, ..., all dimensions but the last counted through in order) at most 8 rows name the same one
Outputs:
- quant_codes: bfloat16 [16, 8, 4, 8, 32, 2112], P(None, 'serve', 'train')
- block_scales: float32 [16, 8, 4, 8, 2112], P(None, 'serve', 'train')
Inputs may be any that keep to these rules, and one draw needn't show every extreme that they name: For every layer l: row_offset[l, 0] = 0 and row_offset[l, 4] = 7168; every other row_offset[l, t] lies 1 to 32 rows above or below t * 1792, never on it; in every layer one entry lies exactly 32 rows above and another exactly 32 rows below; layer 1 has the opposite sign of layer 0 at every such entry. `block_group`: within each aligned block of 56 entries (one training device's blocks of one layer), no group is named more than 8 times; some group reaches 8 in some of them.
All inputs are finite; a program needn't handle non-finite values.
Results may differ from a plain program's by a relative error of at most 0.001.
Values may be sent and summed in bfloat16 or wider, within the bound.
A program may use at most 128 MiB of HBM per device.

v0:
```python
import jax
import jax.numpy as jnp
from jax import lax
from jax.sharding import PartitionSpec as P

BLOCK = 32
SHIFT = 32


def padded_2(cells, sides, width):
    for axis, dim in sides:
        count = lax.axis_size(axis)
        ends = count - 1
        head = lax.slice_in_dim(cells, 0, width, axis=dim)
        tail = lax.slice_in_dim(cells, cells.shape[dim] - width, cells.shape[dim], axis=dim)
        cells = jnp.concatenate(
            [
                lax.ppermute(tail, axis, [(i, (i + 1) % count) for i in range(ends)]),
                cells,
                lax.ppermute(head, axis, [((i + 1) % count, i) for i in range(ends)]),
            ],
            axis=dim,
        )
    return cells


def shards(train_weights, row_offset, block_group):
    train_n = lax.axis_size("train")
    serve_n = lax.axis_size("serve")
    train_idx = lax.axis_index("train")
    buffer_len = train_weights.shape[1]
    rows_dev = buffer_len - 2 * SHIFT
    blocks_dev = block_group.shape[1]
    slots_n = (blocks_dev + serve_n - 1) // serve_n + 1
    entries = jnp.arange(train_n + 1, dtype=jnp.int32)
    position = jnp.arange(blocks_dev, dtype=jnp.int32)
    earlier = position[None, :] < position[:, None]
    slot_range = jnp.arange(serve_n * slots_n, dtype=jnp.int32)
    group_ids = block_group[:, :, 0]
    layer_count = train_weights.shape[0]
    columns = train_weights.shape[2]
    first_row = (
        jnp.sum(jnp.where(entries[None, :] == train_idx, row_offset, 0), axis=1)
        - train_idx * rows_dev
    )
    next_row = (
        jnp.sum(jnp.where(entries[None, :] == train_idx + 1, row_offset, 0), axis=1)
        - train_idx * rows_dev
    )
    padded = padded_2(train_weights, (("train", 1),), SHIFT)
    left_rows = padded[:, :SHIFT]
    right_rows = padded[:, SHIFT + buffer_len :]
    own_rows = padded[:, 2 * SHIFT : 2 * SHIFT + rows_dev]
    filler = jnp.zeros((layer_count, rows_dev - SHIFT, columns), train_weights.dtype)
    left_full = jnp.concatenate([left_rows, filler], axis=1)
    right_full = jnp.concatenate([filler, right_rows], axis=1)
    row_pos = jnp.arange(rows_dev, dtype=jnp.int32)[None, :, None]
    joined = jnp.where(
        row_pos < first_row[:, None, None],
        left_full,
        jnp.where(row_pos >= next_row[:, None, None], right_full, own_rows),
    )
    blocks = joined.reshape(layer_count, blocks_dev, BLOCK, columns)
    same_group = group_ids[:, :, None] == group_ids[:, None, :]
    order_in = jnp.sum((same_group & earlier[None]).astype(jnp.int32), axis=2)
    slot_id = group_ids * slots_n + order_in
    onehot = slot_id[:, None, :] == slot_range[None, :, None]
    absmax = jnp.max(jnp.abs(blocks.astype(jnp.float32)), axis=2, keepdims=True)
    divisor = jnp.maximum(absmax, 0.25)
    coded = (blocks.astype(jnp.float32) / divisor).astype(jnp.bfloat16)
    codes_sent = jnp.einsum(
        "gqj,gjrc->gqrc", onehot.astype(jnp.bfloat16), coded, preferred_element_type=jnp.float32
    ).astype(jnp.bfloat16)
    codes_sent = codes_sent.reshape(layer_count, serve_n, slots_n, BLOCK, columns)
    scale_sent = jnp.einsum(
        "gqj,gjrc->gqrc", onehot.astype(jnp.float32), divisor, precision=lax.Precision.HIGHEST
    )
    scale_sent = scale_sent.reshape(layer_count, serve_n, slots_n, 1, columns)
    quant_codes = lax.all_to_all(codes_sent, "serve", split_axis=1, concat_axis=4, tiled=True)
    block_scale = lax.all_to_all(scale_sent, "serve", split_axis=1, concat_axis=4, tiled=True)
    return (
        quant_codes.reshape(layer_count, 1, 1, slots_n, BLOCK, -1),
        block_scale.reshape(layer_count, 1, 1, slots_n, -1),
    )


def solution(mesh):
    return jax.shard_map(
        shards,
        mesh=mesh,
        in_specs=(P(None, "train", "serve"), P(), P(None, "train", None)),
        out_specs=(
            P(None, "serve", "train", None, None, None),
            P(None, "serve", "train", None, None),
        ),
        check_vma=False,
    )
```

profile of v0, /device:TPU:0, one launch (start us, length us, event | category | flops | bytes accessed | tf_op | source)
XLA Modules:
  0.0 487.3 jit_solution(8023000411100837365)
XLA Ops:
  0.6 2.0 fusion.10
  2.6 0.5 copy.42
  3.1 1.3 collective-permute-start.1
  4.4 0.5 copy.41
  4.9 5.6 %collective-permute-start = (bf16[16,32,264]{2,1,0:T(8,128)(2,1)S(1)}, bf16[16,32,264]{2,1,0:T(8,128)(2,1)S(1)}, u32[]{:S(2)}, u32[]{:S(2)}) collective-permute-start(bf16[16,32,264]{2,1,0:T(8,128)(2,1)S(1)} %copy.41), channel_id=1, source_target_pairs={{0,8},{8,16},{16,24},{1,9},{9,17},{17,25},{2,10},{10,18},{18,26},{... | collective-permute-start | bytes 811016 | tf_op jit(solution)/shard_map/ppermute | solution.py:18
  10.6 0.8 select_reduce_fusion.1
  11.4 0.1 iota_compare_fusion.2
  11.5 0.1 iota_compare_fusion.3
  11.6 1.3 convert_reduce_fusion
  12.8 12.9 %slice.11 = bf16[16,1792,264]{1,2,0:T(8,128)(2,1)} slice(bf16[16,1856,264]{1,2,0:T(8,128)(2,1)} %param.3), slice={[0:16], [32:1824], [0:264]} | slice | bytes 30277632 | tf_op jit(solution)/shard_map/slice | solution.py:53
  25.8 0.0 copy-start
  25.8 24.4 %copy.43 = bf16[16,1792,264]{2,1,0:T(8,128)(2,1)} copy(bf16[16,1792,264]{1,2,0:T(8,128)(2,1)} %slice.11) | data formatting | bytes 30277632
  50.2 0.0 copy-done
  50.2 0.0 collective-permute-done.1
  50.2 0.0 collective-permute-done
  50.2 16.9 %select_select_fusion = bf16[16,1792,264]{2,1,0:T(8,128)(2,1)S(1)} fusion(bf16[16,1792,264]{2,1,0:T(8,128)(2,1)} %copy.43, bf16[16,32,264]{2,1,0:T(8,128)(2,1)S(1)} %collective-permute-done.1, bf16[16,32,264]{2,1,0:T(8,128)(2,1)S(1)} %collective-permute-done, pred[16,1792]{1,0:T(8,128)(4,1)S(1)} %iota_compare_fusion.2, pred[16,1792]{1,0:T(8,128)(4,1)S(1)} %iota_compare_fusion.3), kind=kLoop, calls=%fused_computation.7 | loop fusion | flops 15138816 | bytes 30875648 | tf_op jit(solution)/shard_map/jit(_where)/select_n | solution.py:58
  67.1 9.2 %fusion = f32[16,56,264]{2,1,0:T(8,128)S(1)} fusion(bf16[16,56,32,264]{3,2,1,0:T(8,128)(2,1)S(1)} %bitcast.28), kind=kLoop, calls=%fused_computation.2 | loop fusion | flops 22471680 | bytes 16084992 | tf_op jit(solution)/shard_map/reduce_max | solution.py:68
  76.3 0.1 broadcast_maximum_fusion
  76.4 11.9 %fusion.1 = bf16[16,56,32,264]{3,2,1,0:T(8,128)(2,1)} fusion(bf16[16,56,32,264]{3,2,1,0:T(8,128)(2,1)S(1)} %bitcast.29, f32[16,56,264]{2,1,0:T(8,128)S(1)} %broadcast_maximum_fusion), kind=kLoop, calls=%fused_computation.3 | loop fusion | flops 22708224 | bytes 31223808 | tf_op jit(solution)/shard_map/convert_element_type | solution.py:70
  88.3 1.1 convolution_bitcast_fusion
  89.4 1.2 copy.36
  90.7 4.2 all-to-all-start.1
  94.8 24.3 %convert_bitcast_fusion = bf16[16,8,8,32,264]{4,2,1,3,0:T(8,128)(2,1)} fusion(bf16[16,56,32,264]{3,2,1,0:T(8,128)(2,1)} %fusion.1, s32[16,56]{1,0:T(8,128)S(1)} %multiply_add_fusion), kind=kOutput, calls=%fused_computation.4 | convolution fusion | flops 977592320 | bytes 32443904 | tf_op jit(solution)/shard_map/gqj,gjrc->gqrc/dot_general | solution.py:71
  119.1 22.9 %copy.34 = bf16[16,8,8,32,264]{4,2,3,0,1:T(8,128)(2,1)} copy(bf16[16,8,8,32,264]{4,2,1,3,0:T(8,128)(2,1)} %convert_bitcast_fusion) | data formatting | bytes 34603008 | tf_op jit(solution)/shard_map/reshape | solution.py:74
  142.1 0.0 all-to-all-done.1
  142.1 6.6 %all-to-all-start = ((bf16[16,8,8,32,264]{4,2,3,0,1:T(8,128)(2,1)}), bf16[16,8,8,32,264]{4,2,3,0,1:T(8,128)(2,1)}, u32[]{:S(2)}, u32[]{:S(2)}) async-start(bf16[16,8,8,32,264]{4,2,3,0,1:T(8,128)(2,1)} %copy.34), calls=%async_computation | async-start | bytes 50331648 | tf_op jit(solution)/shard_map/all_to_all | solution.py:79
  148.7 0.9 copy.37
  149.6 1.5 reshape.116
  151.1 271.4 %all-to-all-done = bf16[16,8,8,32,264]{4,2,3,0,1:T(8,128)(2,1)} async-done(((bf16[16,8,8,32,264]{4,2,3,0,1:T(8,128)(2,1)}), bf16[16,8,8,32,264]{4,2,3,0,1:T(8,128)(2,1)}, u32[]{:S(2)}, u32[]{:S(2)}) %all-to-all-start) | async-done | bytes 17301536 | tf_op jit(solution)/shard_map/all_to_all | solution.py:79
  422.5 27.8 %copy.35 = bf16[16,1,8,32,8,264]{5,4,3,2,0,1:T(8,128)(2,1)} copy(bf16[16,1,8,32,8,264]{5,2,3,0,4,1:T(8,128)(2,1)} %bitcast.7) | data formatting | bytes 34603008 | tf_op jit(solution)/shard_map/all_to_all | solution.py:79
  450.2 37.0 %reshape.114 = bf16[16,1,1,8,32,2112]{5,4,3,0,2,1:T(8,128)(2,1)} reshape(bf16[16,1,8,32,8,264]{5,4,3,2,0,1:T(8,128)(2,1)} %copy.35) | data formatting | bytes 34603008 | tf_op jit(solution)/shard_map/reshape | solution.py:82
  (5 shorter events, 0.0 us)
Async XLA Ops:
  3.1 47.1 %collective-permute-start.1 = (bf16[16,32,264]{2,1,0:T(8,128)(2,1)S(1)}, bf16[16,32,264]{2,1,0:T(8,128)(2,1)S(1)}, u32[]{:S(2)}, u32[]{:S(2)}) collective-permute-start(bf16[16,32,264]{2,1,0:T(8,128)(2,1)S(1)} %copy.42), channel_id=1, source_target_pairs={{8,0},{16,8},{24,16},{9,1},{17,9},{25,17},{10,2},{18,10},{26,18},{... | collective-permute-start | bytes 811016 | tf_op jit(solution)/shard_map/ppermute | solution.py:20
  4.9 45.3 %collective-permute-start = (bf16[16,32,264]{2,1,0:T(8,128)(2,1)S(1)}, bf16[16,32,264]{2,1,0:T(8,128)(2,1)S(1)}, u32[]{:S(2)}, u32[]{:S(2)}) collective-permute-start(bf16[16,32,264]{2,1,0:T(8,128)(2,1)S(1)} %copy.41), channel_id=1, source_target_pairs={{0,8},{8,16},{16,24},{1,9},{9,17},{17,25},{2,10},{10,18},{18,26},{... | collective-permute-start | bytes 811016 | tf_op jit(solution)/shard_map/ppermute | solution.py:18
  25.8 24.4 %copy-start = (s32[16,56,1]{1,2,0:T(1,128)S(1)}, s32[16,56,1]{1,2,0:T(1,128)}, u32[]{:S(2)}) copy-start(s32[16,56,1]{1,2,0:T(1,128)} %param.5) | copy-start | bytes 10756
  90.7 51.4 %all-to-all-start.1 = ((f32[16,8,8,1,264]{4,2,0,3,1:T(8,128)}), f32[16,8,8,1,264]{4,2,0,3,1:T(8,128)S(1)}, u32[]{:S(2)}, u32[]{:S(2)}) async-start(f32[16,8,8,1,264]{4,2,0,3,1:T(8,128)} %copy.36), calls=%async_computation.1 | async-start | bytes 3145728 | tf_op jit(solution)/shard_map/all_to_all | solution.py:80
  142.1 280.4 %all-to-all-start = ((bf16[16,8,8,32,264]{4,2,3,0,1:T(8,128)(2,1)}), bf16[16,8,8,32,264]{4,2,3,0,1:T(8,128)(2,1)}, u32[]{:S(2)}, u32[]{:S(2)}) async-start(bf16[16,8,8,32,264]{4,2,3,0,1:T(8,128)(2,1)} %copy.34), calls=%async_computation | async-start | bytes 50331648 | tf_op jit(solution)/shard_map/all_to_all | solution.py:79
where the time goes:
time: 490 us; the launch traced here: 487 us
  waiting for transfers between devices  271 us (55%)
  local copies, waits for them, and re-layouts  132 us (27%)
  other arithmetic  40.3 us (8%)
  matrix products  25.4 us (5%)
  starting transfers between devices  17.7 us (4%)
    all_to_all x1, waiting for transfers between devices, shards(): lax.all_to_all(codes_sent, 'serve', split_axis=1, concat_axis=4, tiled=True)  271 us
    reshape x1, local copies, waits for them, and re-layouts, shards(): quant_codes.reshape(layer_count, 1, 1, slots_n, BLOCK, -1)  37 us
    all_to_all x1, local copies, waits for them, and re-layouts, shards(): lax.all_to_all(codes_sent, 'serve', split_axis=1, concat_axis=4, tiled=True)  27.8 us
    unnamed x5, local copies, waits for them, and re-layouts  25.4 us
    dot_general x1, matrix products, shards(): jnp.einsum('gqj,gjrc->gqrc', onehot.astype(jnp.bfloat16), coded, preferre...  24.3 us
    reshape x1, local copies, waits for them, and re-layouts, shards(): codes_sent.reshape(layer_count, serve_n, slots_n, BLOCK, columns)  22.9 us
    select_n x1, other arithmetic, shards(): jnp.where(row_pos < first_row[:, None, None], left_full, jnp.where(row_po...  16.9 us
    slice x1, local copies, waits for them, and re-layouts, shards(): own_rows = padded[:, 2 * SHIFT:2 * SHIFT + rows_dev]  12.9 us
  transfers between devices with their start and end apart: 4, of which 1 were waited for; matrix products, arithmetic and copies ran while one was open for 18% of the time, Pallas kernels for 0%

commit v1 on v0

v1 whole, which is shorter than its diff:
```python
import functools

import jax
import jax.numpy as jnp
from jax import lax
from jax.experimental import pallas as pl
from jax.experimental.pallas import tpu as pltpu
from jax.sharding import PartitionSpec as P

BLOCK = 32
SHIFT = 32
LANES = 128
PAIR = 2
CHUNKS = 4


def turned(values):
    return jnp.transpose(values.astype(jnp.float32))


def pack_kernel(base, slots_n, group_ref, order_ref, first_ref, next_ref, wt_ref, left_ref, right_ref, out_ref, rem_ref, w_ref):
    step = pl.program_id(0)
    columns, buffer_len = wt_ref.shape[1:]
    full = columns // LANES
    rem = columns - full * LANES
    blocks_dev = group_ref.shape[1]
    groups = out_ref.shape[0]
    row = lax.broadcasted_iota(jnp.int32, (BLOCK, columns), 0)
    for sub in range(PAIR):
        layer = (base + step) * PAIR + sub
        for low in range(0, buffer_len, LANES):
            high = min(low + LANES, buffer_len)
            w_ref[sub, low:high, :] = turned(wt_ref[sub, :, low:high]).astype(w_ref.dtype)

        def place(j, block, sub=sub, layer=layer):
            g = group_ref[layer, j]
            k = order_ref[layer, j]
            for t in range(full):
                out_ref[g, 0, (sub * slots_n + k) * full + t] = block[:, t * LANES : (t + 1) * LANES]
            if rem:
                rem_ref[g, sub * slots_n + k, :, 0:rem] = block[:, full * LANES :]

        def inner(j, carry, sub=sub, place=place):
            start = pl.multiple_of(SHIFT + j * BLOCK, BLOCK)
            place(j, w_ref[sub, pl.ds(start, BLOCK), :])
            return carry

        lax.fori_loop(1, blocks_dev - 1, inner, 0, unroll=6 if (blocks_dev - 2) % 6 == 0 else 2)
        head = jnp.where(
            row < first_ref[layer],
            left_ref[sub].astype(jnp.float32),
            w_ref[sub, SHIFT : SHIFT + BLOCK, :].astype(jnp.float32),
        )
        place(0, head.astype(out_ref.dtype))
        last = (blocks_dev - 1) * BLOCK
        tail = jnp.where(
            row + last >= next_ref[layer],
            right_ref[sub].astype(jnp.float32),
            w_ref[sub, SHIFT + last : SHIFT + last + BLOCK, :].astype(jnp.float32),
        )
        place(blocks_dev - 1, tail.astype(out_ref.dtype))
    if rem:
        lane = lax.broadcasted_iota(jnp.int32, (BLOCK, LANES), 1)

        def gather(g, carry):
            tile = rem_ref[g, 0].astype(jnp.float32)
            for i in range(1, PAIR * slots_n):
                moved = pltpu.roll(rem_ref[g, i].astype(jnp.float32), i * rem, 1)
                tile = jnp.where(lane >= i * rem, moved, tile)
            out_ref[g, 0, PAIR * slots_n * full] = tile.astype(out_ref.dtype)
            return carry

        lax.fori_loop(0, groups, gather, 0)


def unpack_kernel(base, slots_n, columns, count_ref, *refs):
    recv_ref, codes_ref, scale_ref, rem_code, rem_scale = refs[0], *refs[-4:]
    step = pl.program_id(0)
    full = columns // LANES
    rem = columns - full * LANES
    sources = recv_ref.shape[0]
    width = codes_ref.shape[3]
    tiles = -(-width // LANES)

    def scaled(values):
        values = values.astype(jnp.float32)
        divisor = jnp.maximum(jnp.max(jnp.abs(values), axis=0, keepdims=True), 0.25)
        return values * (1.0 / divisor), divisor

    if rem:
        for s in range(sources):
            rem_code[s], rem_scale[s] = scaled(recv_ref[s, 0, PAIR * slots_n * full])
    lane = lax.broadcasted_iota(jnp.int32, (BLOCK, LANES), 1)
    lane_row = lax.broadcasted_iota(jnp.int32, (1, LANES), 1)

    for sub in range(PAIR):
        count = count_ref[(base + step) * PAIR + sub]
        for k in range(slots_n):
            i = sub * slots_n + k

            @pl.when(k < count)
            def _():
                parts = [None] * tiles

                def put(tile, low, code, scale):
                    if tile >= tiles:
                        return
                    if parts[tile] is None:
                        parts[tile] = (code, scale)
                    else:
                        before = parts[tile]
                        parts[tile] = (
                            jnp.where(lane >= low, code, before[0]),
                            jnp.where(lane_row >= low, scale, before[1]),
                        )

                def flush(below):
                    for tile in range(below):
                        if parts[tile] is not None:
                            code, scale = parts[tile]
                            end = min(width, (tile + 1) * LANES)
                            size = end - tile * LANES
                            codes_ref[sub, k, :, tile * LANES : end] = code[:, :size].astype(codes_ref.dtype)
                            scale_ref[sub, k : k + 1, tile * LANES : end] = scale[:, :size]
                            parts[tile] = None

                for s in range(sources):
                    for t in range(full + (1 if rem else 0)):
                        start = s * columns + t * LANES
                        size = LANES if t < full else rem
                        low = start % LANES
                        if t < full:
                            code, scale = scaled(recv_ref[s, 0, i * full + t])
                            turn = low
                        else:
                            code, scale = rem_code[s], rem_scale[s]
                            turn = (low - i * rem) % LANES
                        if turn:
                            code = pltpu.roll(code, turn, 1)
                            scale = pltpu.roll(scale, turn, 1)
                        tile = start // LANES
                        put(tile, low, code, scale)
                        if low + size > LANES:
                            put(tile + 1, 0, code, scale)
                        flush((start + size) // LANES)
                flush(tiles)

            @pl.when(k >= count)
            def _():
                codes_ref[sub, k] = jnp.zeros((BLOCK, width), codes_ref.dtype)
                scale_ref[sub, k : k + 1] = jnp.zeros((1, width), scale_ref.dtype)


def shards(train_weights, row_offset, block_group):
    train_n = lax.axis_size("train")
    serve_n = lax.axis_size("serve")
    train_idx = lax.axis_index("train")
    serve_idx = lax.axis_index("serve")
    layers, buffer_len, columns = train_weights.shape
    rows_dev = buffer_len - 2 * SHIFT
    blocks_dev = block_group.shape[1]
    slots_n = (blocks_dev + serve_n - 1) // serve_n + 1
    full = columns // LANES
    rem = columns - full * LANES
    assert PAIR * slots_n * rem <= LANES and layers % PAIR == 0
    pieces = PAIR * slots_n * full + (1 if rem else 0)
    pairs = layers // PAIR
    chunks = CHUNKS if pairs % CHUNKS == 0 else 1
    per = pairs // chunks
    width = columns * serve_n
    dtype = train_weights.dtype

    entries = jnp.arange(train_n + 1, dtype=jnp.int32)
    position = jnp.arange(blocks_dev, dtype=jnp.int32)
    earlier = position[None, :] < position[:, None]
    group_ids = block_group[:, :, 0]
    first_row = jnp.sum(jnp.where(entries[None, :] == train_idx, row_offset, 0), axis=1) - train_idx * rows_dev
    next_row = jnp.sum(jnp.where(entries[None, :] == train_idx + 1, row_offset, 0), axis=1) - train_idx * rows_dev
    same_group = group_ids[:, :, None] == group_ids[:, None, :]
    order_in = jnp.sum((same_group & earlier[None]).astype(jnp.int32), axis=2)
    count = jnp.sum((group_ids == serve_idx).astype(jnp.int32), axis=1)

    ends = train_n - 1
    up = [(i, i + 1) for i in range(ends)]
    down = [(i + 1, i) for i in range(ends)]
    turned_weights = jnp.swapaxes(train_weights, 1, 2)
    received = []
    for c in range(chunks):
        low, high = c * per * PAIR, (c + 1) * per * PAIR
        left = lax.ppermute(train_weights[low:high, buffer_len - SHIFT :], "train", up)
        right = lax.ppermute(train_weights[low:high, :SHIFT], "train", down)
        sent = pl.pallas_call(
            functools.partial(pack_kernel, c * per, slots_n),
            grid_spec=pltpu.PrefetchScalarGridSpec(
                num_scalar_prefetch=4,
                grid=(per,),
                in_specs=[
                    pl.BlockSpec((PAIR, columns, buffer_len), lambda p, *_, c=c: (c * per + p, 0, 0)),
                    pl.BlockSpec((PAIR, SHIFT, columns), lambda p, *_: (p, 0, 0)),
                    pl.BlockSpec((PAIR, SHIFT, columns), lambda p, *_: (p, 0, 0)),
                ],
                out_specs=pl.BlockSpec((serve_n, 1, pieces, BLOCK, LANES), lambda p, *_: (0, p, 0, 0, 0)),
                scratch_shapes=[pltpu.VMEM((serve_n, PAIR * slots_n, BLOCK, LANES), dtype), pltpu.VMEM((PAIR, buffer_len, columns), dtype)],
            ),
            out_shape=jax.ShapeDtypeStruct((serve_n, per, pieces, BLOCK, LANES), dtype),
            cost_estimate=pl.CostEstimate(flops=0, bytes_accessed=30_000_000 // chunks, transcendentals=0),
            name=f"pack{c}",
        )(group_ids, order_in, first_row, next_row, turned_weights, left, right)
        received.append(lax.all_to_all(sent, "serve", split_axis=0, concat_axis=0, tiled=True))

    outs = None
    for c in range(chunks):
        held = () if outs is None else outs
        outs = pl.pallas_call(
            functools.partial(unpack_kernel, c * per, slots_n, columns),
            grid_spec=pltpu.PrefetchScalarGridSpec(
                num_scalar_prefetch=1,
                grid=(per,),
                in_specs=[pl.BlockSpec((serve_n, 1, pieces, BLOCK, LANES), lambda p, *_: (0, p, 0, 0, 0))]
                + [pl.BlockSpec(memory_space=pl.ANY)] * len(held),
                out_specs=[
                    pl.BlockSpec((PAIR, slots_n, BLOCK, width), lambda p, *_, c=c: (c * per + p, 0, 0, 0)),
                    pl.BlockSpec((PAIR, slots_n, width), lambda p, *_, c=c: (c * per + p, 0, 0)),
                ],
                scratch_shapes=[
                    pltpu.VMEM((serve_n, BLOCK, LANES), jnp.float32),
                    pltpu.VMEM((serve_n, 1, LANES), jnp.float32),
                ],
            ),
            out_shape=[
                jax.ShapeDtypeStruct((layers, slots_n, BLOCK, width), dtype),
                jax.ShapeDtypeStruct((layers, slots_n, width), jnp.float32),
            ],
            input_output_aliases={2: 0, 3: 1} if held else {},
            cost_estimate=pl.CostEstimate(flops=0, bytes_accessed=40_000_000 // chunks, transcendentals=0),
            name=f"unpack{c}",
        )(count, received[c], *held)
    codes, scales = outs
    return (
        codes.reshape(layers, 1, 1, slots_n, BLOCK, width),
        scales.reshape(layers, 1, 1, slots_n, width),
    )


def solution(mesh):
    return jax.shard_map(
        shards,
        mesh=mesh,
        in_specs=(P(None, "train", "serve"), P(), P(None, "train", None)),
        out_specs=(
            P(None, "serve", "train", None, None, None),
            P(None, "serve", "train", None, None),
        ),
        check_vma=False,
    )
```

time: 490 us -> 254 us (0.52)
  waiting for transfers between devices: 271 us -> 135 us
  local copies, waits for them, and re-layouts: 132 us -> 5.92 us
  Pallas kernels: 0 us -> 69.3 us
  other arithmetic: 40.3 us -> 2.5 us
  matrix products: 25.4 us -> 0 us
  starting transfers between devices: 17.7 us -> 39.1 us
    all_to_all x2 -> x4, waiting for transfers between devices: 271 us -> 116 us  [shards(): lax.all_to_all(sent, 'serve', split_axis=0, concat_axis=0, tiled=True)]
    pallas_call x0 -> x8, Pallas kernels: none -> 69.3 us  [the longest x4 37.7 us: shards(): pl.pallas_call(functools.partial(pack_kernel, c * per, slots_n), grid_spe...]
    reshape x4 -> x0, local copies, waits for them, and re-layouts: 62.7 us -> none  [the longest x1 37 us: shards(): quant_codes.reshape(layer_count, 1, 1, slots_n, BLOCK, -1)]
    all_to_all x2 -> x0, local copies, waits for them, and re-layouts: 28.7 us -> none  [the longest x1 27.8 us: shards(): lax.all_to_all(codes_sent, 'serve', split_axis=1, concat_axis=4, tiled=True)]
    dot_general x2 -> x0, matrix products: 25.4 us -> none  [the longest x1 24.3 us: shards(): jnp.einsum('gqj,gjrc->gqrc', onehot.astype(jnp.bfloat16), coded, preferre...]
    unnamed x5 -> x30, local copies, waits for them, and re-layouts: 25.4 us -> 3.9 us
    ppermute x2 -> x8, waiting for transfers between devices: 0.01 us -> 19.5 us  [the longest x4 16.2 us: shards(): right = lax.ppermute(train_weights[low:high, :SHIFT], 'train', down)]
    select_n x1 -> x0, other arithmetic: 16.9 us -> none  [shards(): jnp.where(row_pos < first_row[:, None, None], left_full, jnp.where(row_po...]
  transfers between devices with their start and end apart: 4 -> 12, of which waited for: 1 -> 11; matrix products, arithmetic and copies ran while one was open for 18% -> 1% of each run, Pallas kernels for 0% -> 21%
where the time goes in v1:
time: 254 us; the launch traced here: 253 us
  waiting for transfers between devices  135 us (53%)
  Pallas kernels  69.3 us (27%)
  starting transfers between devices  39.1 us (15%)
  local copies, waits for them, and re-layouts  5.92 us (2%)
    all_to_all x4, waiting for transfers between devices, shards(): lax.all_to_all(sent, 'serve', split_axis=0, concat_axis=0, tiled=True)  116 us
    pallas_call x4, Pallas kernels, shards(): pl.pallas_call(functools.partial(pack_kernel, c * per, slots_n), grid_spe...  37.7 us
    pallas_call x4, Pallas kernels, shards(): pl.pallas_call(functools.partial(unpack_kernel, c * per, slots_n, columns...  31.6 us
    all_to_all x4, starting transfers between devices, shards(): lax.all_to_all(sent, 'serve', split_axis=0, concat_axis=0, tiled=True)  18.5 us
    ppermute x4, waiting for transfers between devices, shards(): right = lax.ppermute(train_weights[low:high, :SHIFT], 'train', down)  16.2 us
    ppermute x4, starting transfers between devices, shards(): lax.ppermute(train_weights[low:high, buffer_len - SHIFT:], 'train', up)  15.4 us
    ppermute x4, starting transfers between devices, shards(): right = lax.ppermute(train_weights[low:high, :SHIFT], 'train', down)  5.17 us
  transfers between devices with their start and end apart: 12, of which 11 were waited for; matrix products, arithmetic and copies ran while one was open for 1% of the time, Pallas kernels for 21%

profile of v1, /device:TPU:0, one launch (start us, length us, event | category | flops | bytes accessed | tf_op | source)
XLA Modules:
  0.0 252.9 jit_solution(11573173764627536501)
XLA Ops:
  0.7 2.0 fusion
  2.7 0.2 copy.37
  2.9 5.0 %collective-permute-start.6 = (bf16[4,32,264]{2,1,0:T(8,128)(2,1)S(1)}, bf16[4,32,264]{2,1,0:T(8,128)(2,1)S(1)}, u32[]{:S(2)}, u32[]{:S(2)}) collective-permute-start(bf16[4,32,264]{2,1,0:T(8,128)(2,1)S(1)} %copy.37), channel_id=1, source_target_pairs={{0,8},{8,16},{16,24},{1,9},{9,17},{17,25},{2,10},{10,18},{18,26},{... | collective-permute-start | bytes 202760 | tf_op jit(solution)/shard_map/ppermute | solution.py:190
  7.8 0.2 copy.38
  8.0 1.3 collective-permute-start.7
  9.4 0.1 select_reduce_fusion
  9.4 0.6 broadcast_subtract_fusion
  10.0 1.1 convert_reduce_fusion.order_ref
  11.2 3.3 %collective-permute-done.7.right_ref = bf16[4,32,264]{2,1,0:T(8,128)(2,1)S(1)} collective-permute-done((bf16[4,32,264]{2,1,0:T(8,128)(2,1)S(1)}, bf16[4,32,264]{2,1,0:T(8,128)(2,1)S(1)}, u32[]{:S(2)}, u32[]{:S(2)}) %collective-permute-start.7) | collective-permute-done | bytes 67616 | tf_op jit(solution)/shard_map/ppermute | solution.py:191
  14.5 0.6 copy-done.3
  15.1 9.4 %pack0.1 = bf16[8,2,33,32,128]{4,3,2,1,0:T(8,128)(2,1)} custom-call(s32[16,56]{1,0:T(8,128)} %bitcast.14, s32[16,56]{1,0:T(8,128)} %convert_reduce_fusion.order_ref, s32[16]{0:T(128)} %get-tuple-element.33.first_ref, s32[16]{0:T(128)} %get-tuple-element.32.next_ref, bf16[16,264,1856]{2,1,0:T(8,128)(2,1)} %bitcast.8, bf16[4,32,264]{2,1,0:T(8,128)(2,1)} %copy-done.2, ...), custom_call_target="tpu_custom_call" | custom-call | bytes 7500000 | tf_op jit(solution)/shard_map/pack0/pallas_call | solution.py:192
  24.5 4.6 %all-to-all-start.3 = ((bf16[8,2,33,32,128]{4,3,2,1,0:T(8,128)(2,1)}), bf16[8,2,33,32,128]{4,3,2,1,0:T(8,128)(2,1)}, u32[]{:S(2)}, u32[]{:S(2)}) async-start(bf16[8,2,33,32,128]{4,3,2,1,0:T(8,128)(2,1)} %pack0.1), calls=%async_computation.3 | async-start | bytes 8650752 | tf_op jit(solution)/shard_map/all_to_all | solution.py:209
  29.1 0.2 copy.35
  29.3 3.5 %collective-permute-start.4 = (bf16[4,32,264]{2,1,0:T(8,128)(2,1)S(1)}, bf16[4,32,264]{2,1,0:T(8,128)(2,1)S(1)}, u32[]{:S(2)}, u32[]{:S(2)}) collective-permute-start(bf16[4,32,264]{2,1,0:T(8,128)(2,1)S(1)} %copy.35), channel_id=1, source_target_pairs={{0,8},{8,16},{16,24},{1,9},{9,17},{17,25},{2,10},{10,18},{18,26},{... | collective-permute-start | bytes 202760 | tf_op jit(solution)/shard_map/ppermute | solution.py:190
  32.8 0.2 copy.36
  33.0 1.3 collective-permute-start.5
  34.3 1.1 collective-permute-done.4.left_ref
  35.4 4.3 %collective-permute-done.5.right_ref = bf16[4,32,264]{2,1,0:T(8,128)(2,1)S(1)} collective-permute-done((bf16[4,32,264]{2,1,0:T(8,128)(2,1)S(1)}, bf16[4,32,264]{2,1,0:T(8,128)(2,1)S(1)}, u32[]{:S(2)}, u32[]{:S(2)}) %collective-permute-start.5) | collective-permute-done | bytes 67616 | tf_op jit(solution)/shard_map/ppermute | solution.py:191
  39.6 0.6 copy-done.8
  40.3 9.4 %pack1.1 = bf16[8,2,33,32,128]{4,3,2,1,0:T(8,128)(2,1)} custom-call(s32[16,56]{1,0:T(8,128)} %bitcast.15, s32[16,56]{1,0:T(8,128)} %convert_reduce_fusion.order_ref, s32[16]{0:T(128)} %get-tuple-element.33.first_ref, s32[16]{0:T(128)} %get-tuple-element.32.next_ref, bf16[16,264,1856]{2,1,0:T(8,128)(2,1)} %bitcast.9, bf16[4,32,264]{2,1,0:T(8,128)(2,1)} %copy-done.5, ...), custom_call_target="tpu_custom_call" | custom-call | bytes 7500000 | tf_op jit(solution)/shard_map/pack1/pallas_call | solution.py:192
  49.7 29.9 %all-to-all-done.3.refs_0_ = bf16[8,2,33,32,128]{4,3,2,1,0:T(8,128)(2,1)} async-done(((bf16[8,2,33,32,128]{4,3,2,1,0:T(8,128)(2,1)}), bf16[8,2,33,32,128]{4,3,2,1,0:T(8,128)(2,1)}, u32[]{:S(2)}, u32[]{:S(2)}) %all-to-all-start.3) | async-done | bytes 4325408 | tf_op jit(solution)/shard_map/all_to_all | solution.py:209
  79.6 4.6 %all-to-all-start.2 = ((bf16[8,2,33,32,128]{4,3,2,1,0:T(8,128)(2,1)}), bf16[8,2,33,32,128]{4,3,2,1,0:T(8,128)(2,1)}, u32[]{:S(2)}, u32[]{:S(2)}) async-start(bf16[8,2,33,32,128]{4,3,2,1,0:T(8,128)(2,1)} %pack1.1), calls=%async_computation.2 | async-start | bytes 8650752 | tf_op jit(solution)/shard_map/all_to_all | solution.py:209
  84.2 0.2 copy.33
  84.4 3.5 %collective-permute-start.2 = (bf16[4,32,264]{2,1,0:T(8,128)(2,1)S(1)}, bf16[4,32,264]{2,1,0:T(8,128)(2,1)S(1)}, u32[]{:S(2)}, u32[]{:S(2)}) collective-permute-start(bf16[4,32,264]{2,1,0:T(8,128)(2,1)S(1)} %copy.33), channel_id=1, source_target_pairs={{0,8},{8,16},{16,24},{1,9},{9,17},{17,25},{2,10},{10,18},{18,26},{... | collective-permute-start | bytes 202760 | tf_op jit(solution)/shard_map/ppermute | solution.py:190
  87.9 0.2 copy.34
  88.0 1.3 collective-permute-start.3
  89.3 1.1 collective-permute-done.2.left_ref
  90.5 4.3 %collective-permute-done.3.right_ref = bf16[4,32,264]{2,1,0:T(8,128)(2,1)S(1)} collective-permute-done((bf16[4,32,264]{2,1,0:T(8,128)(2,1)S(1)}, bf16[4,32,264]{2,1,0:T(8,128)(2,1)S(1)}, u32[]{:S(2)}, u32[]{:S(2)}) %collective-permute-start.3) | collective-permute-done | bytes 67616 | tf_op jit(solution)/shard_map/ppermute | solution.py:191
  94.7 0.6 copy-done.9
  95.4 9.4 %pack2.1 = bf16[8,2,33,32,128]{4,3,2,1,0:T(8,128)(2,1)} custom-call(s32[16,56]{1,0:T(8,128)} %bitcast.16, s32[16,56]{1,0:T(8,128)} %convert_reduce_fusion.order_ref, s32[16]{0:T(128)} %get-tuple-element.33.first_ref, s32[16]{0:T(128)} %get-tuple-element.32.next_ref, bf16[16,264,1856]{2,1,0:T(8,128)(2,1)} %bitcast.10, bf16[4,32,264]{2,1,0:T(8,128)(2,1)} %copy-done.6, ...), custom_call_target="tpu_custom_call" | custom-call | bytes 7500000 | tf_op jit(solution)/shard_map/pack2/pallas_call | solution.py:192
  104.8 29.9 %all-to-all-done.2.refs_0_ = bf16[8,2,33,32,128]{4,3,2,1,0:T(8,128)(2,1)} async-done(((bf16[8,2,33,32,128]{4,3,2,1,0:T(8,128)(2,1)}), bf16[8,2,33,32,128]{4,3,2,1,0:T(8,128)(2,1)}, u32[]{:S(2)}, u32[]{:S(2)}) %all-to-all-start.2) | async-done | bytes 4325408 | tf_op jit(solution)/shard_map/all_to_all | solution.py:209
  134.7 4.6 %all-to-all-start.1 = ((bf16[8,2,33,32,128]{4,3,2,1,0:T(8,128)(2,1)}), bf16[8,2,33,32,128]{4,3,2,1,0:T(8,128)(2,1)}, u32[]{:S(2)}, u32[]{:S(2)}) async-start(bf16[8,2,33,32,128]{4,3,2,1,0:T(8,128)(2,1)} %pack2.1), calls=%async_computation.1 | async-start | bytes 8650752 | tf_op jit(solution)/shard_map/all_to_all | solution.py:209
  139.3 0.2 copy.31
  139.5 3.5 %collective-permute-start = (bf16[4,32,264]{2,1,0:T(8,128)(2,1)S(1)}, bf16[4,32,264]{2,1,0:T(8,128)(2,1)S(1)}, u32[]{:S(2)}, u32[]{:S(2)}) collective-permute-start(bf16[4,32,264]{2,1,0:T(8,128)(2,1)S(1)} %copy.31), channel_id=1, source_target_pairs={{0,8},{8,16},{16,24},{1,9},{9,17},{17,25},{2,10},{10,18},{18,26},{... | collective-permute-start | bytes 202760 | tf_op jit(solution)/shard_map/ppermute | solution.py:190
  143.0 0.2 copy.32
  143.2 1.3 collective-permute-start.1
  144.5 1.1 collective-permute-done.left_ref
  145.6 4.3 %collective-permute-done.1.right_ref = bf16[4,32,264]{2,1,0:T(8,128)(2,1)S(1)} collective-permute-done((bf16[4,32,264]{2,1,0:T(8,128)(2,1)S(1)}, bf16[4,32,264]{2,1,0:T(8,128)(2,1)S(1)}, u32[]{:S(2)}, u32[]{:S(2)}) %collective-permute-start.1) | collective-permute-done | bytes 67616 | tf_op jit(solution)/shard_map/ppermute | solution.py:191
  149.9 0.6 copy-done.7
  150.5 9.4 %pack3.1 = bf16[8,2,33,32,128]{4,3,2,1,0:T(8,128)(2,1)} custom-call(s32[16,56]{1,0:T(8,128)} %bitcast.17, s32[16,56]{1,0:T(8,128)} %convert_reduce_fusion.order_ref, s32[16]{0:T(128)} %get-tuple-element.33.first_ref, s32[16]{0:T(128)} %get-tuple-element.32.next_ref, bf16[16,264,1856]{2,1,0:T(8,128)(2,1)} %bitcast.11, bf16[4,32,264]{2,1,0:T(8,128)(2,1)} %copy-done.4, ...), custom_call_target="tpu_custom_call" | custom-call | bytes 7500000 | tf_op jit(solution)/shard_map/pack3/pallas_call | solution.py:192
  159.9 29.9 %all-to-all-done.1.refs_0_ = bf16[8,2,33,32,128]{4,3,2,1,0:T(8,128)(2,1)} async-done(((bf16[8,2,33,32,128]{4,3,2,1,0:T(8,128)(2,1)}), bf16[8,2,33,32,128]{4,3,2,1,0:T(8,128)(2,1)}, u32[]{:S(2)}, u32[]{:S(2)}) %all-to-all-start.1) | async-done | bytes 4325408 | tf_op jit(solution)/shard_map/all_to_all | solution.py:209
  189.8 4.7 %all-to-all-start = ((bf16[8,2,33,32,128]{4,3,2,1,0:T(8,128)(2,1)}), bf16[8,2,33,32,128]{4,3,2,1,0:T(8,128)(2,1)}, u32[]{:S(2)}, u32[]{:S(2)}) async-start(bf16[8,2,33,32,128]{4,3,2,1,0:T(8,128)(2,1)} %pack3.1), calls=%async_computation | async-start | bytes 8650752 | tf_op jit(solution)/shard_map/all_to_all | solution.py:209
  194.6 0.7 convert_reduce_fusion.1.count_ref
  195.3 7.8 %unpack0.1 = (bf16[16,8,32,2112]{3,2,1,0:T(8,128)(2,1)}, f32[16,8,2112]{2,1,0:T(8,128)}) custom-call(s32[16]{0:T(128)} %convert_reduce_fusion.1.count_ref, bf16[8,2,33,32,128]{4,3,2,1,0:T(8,128)(2,1)} %all-to-all-done.3.refs_0_), custom_call_target="tpu_custom_call" | custom-call | bytes 10000000 | tf_op jit(solution)/shard_map/unpack0/pallas_call | solution.py:214
  203.1 8.0 %unpack1.1 = (bf16[16,8,32,2112]{3,2,1,0:T(8,128)(2,1)}, f32[16,8,2112]{2,1,0:T(8,128)}) custom-call(s32[16]{0:T(128)} %convert_reduce_fusion.1.count_ref, bf16[8,2,33,32,128]{4,3,2,1,0:T(8,128)(2,1)} %all-to-all-done.2.refs_0_, bf16[16,8,32,2112]{3,2,1,0:T(8,128)(2,1)} %get-tuple-element.10.refs_1_, ...), custom_call_target="tpu_custom_call", output_to_operand_aliasing={{0}: (2, {}), {1}: (3, {})} | custom-call | bytes 10000000 | tf_op jit(solution)/shard_map/unpack1/pallas_call | solution.py:214
  211.1 7.8 %unpack2.1 = (bf16[16,8,32,2112]{3,2,1,0:T(8,128)(2,1)}, f32[16,8,2112]{2,1,0:T(8,128)}) custom-call(s32[16]{0:T(128)} %convert_reduce_fusion.1.count_ref, bf16[8,2,33,32,128]{4,3,2,1,0:T(8,128)(2,1)} %all-to-all-done.1.refs_0_, bf16[16,8,32,2112]{3,2,1,0:T(8,128)(2,1)} %get-tuple-element.12.refs_1_, ...), custom_call_target="tpu_custom_call", output_to_operand_aliasing={{0}: (2, {}), {1}: (3, {})} | custom-call | bytes 10000000 | tf_op jit(solution)/shard_map/unpack2/pallas_call | solution.py:214
  218.9 26.0 %all-to-all-done.refs_0_ = bf16[8,2,33,32,128]{4,3,2,1,0:T(8,128)(2,1)} async-done(((bf16[8,2,33,32,128]{4,3,2,1,0:T(8,128)(2,1)}), bf16[8,2,33,32,128]{4,3,2,1,0:T(8,128)(2,1)}, u32[]{:S(2)}, u32[]{:S(2)}) %all-to-all-start) | async-done | bytes 4325408 | tf_op jit(solution)/shard_map/all_to_all | solution.py:209
  244.9 8.0 %unpack3.1 = (bf16[16,8,32,2112]{3,2,1,0:T(8,128)(2,1)}, f32[16,8,2112]{2,1,0:T(8,128)}) custom-call(s32[16]{0:T(128)} %convert_reduce_fusion.1.count_ref, bf16[8,2,33,32,128]{4,3,2,1,0:T(8,128)(2,1)} %all-to-all-done.refs_0_, bf16[16,8,32,2112]{3,2,1,0:T(8,128)(2,1)} %get-tuple-element.14.refs_1_, ...), custom_call_target="tpu_custom_call", output_to_operand_aliasing={{0}: (2, {}), {1}: (3, {})} | custom-call | bytes 10000000 | tf_op jit(solution)/shard_map/unpack3/pallas_call | solution.py:214
  (22 shorter events, 0.1 us)
Async XLA Ops:
  0.6 8.7 %copy-start.10 = (s32[16,5]{0,1:T(8,128)S(1)}, s32[16,5]{0,1:T(8,128)}, u32[]{:S(2)}) copy-start(s32[16,5]{0,1:T(8,128)} %param.4) | copy-start | bytes 964
  0.6 9.4 %copy-start = (s32[16,56,1]{1,2,0:T(1,128)S(1)}, s32[16,56,1]{1,2,0:T(1,128)}, u32[]{:S(2)}) copy-start(s32[16,56,1]{1,2,0:T(1,128)} %param.5) | copy-start | bytes 10756
  2.9 8.3 %collective-permute-start.6 = (bf16[4,32,264]{2,1,0:T(8,128)(2,1)S(1)}, bf16[4,32,264]{2,1,0:T(8,128)(2,1)S(1)}, u32[]{:S(2)}, u32[]{:S(2)}) collective-permute-start(bf16[4,32,264]{2,1,0:T(8,128)(2,1)S(1)} %copy.37), channel_id=1, source_target_pairs={{0,8},{8,16},{16,24},{1,9},{9,17},{17,25},{2,10},{10,18},{18,26},{... | collective-permute-start | bytes 202760 | tf_op jit(solution)/shard_map/ppermute | solution.py:190
  8.0 6.5 %collective-permute-start.7 = (bf16[4,32,264]{2,1,0:T(8,128)(2,1)S(1)}, bf16[4,32,264]{2,1,0:T(8,128)(2,1)S(1)}, u32[]{:S(2)}, u32[]{:S(2)}) collective-permute-start(bf16[4,32,264]{2,1,0:T(8,128)(2,1)S(1)} %copy.38), channel_id=1, source_target_pairs={{8,0},{16,8},{24,16},{9,1},{17,9},{25,17},{10,2},{18,10},{26,18},{... | collective-permute-start | bytes 202760 | tf_op jit(solution)/shard_map/ppermute | solution.py:191
  11.2 3.3 %copy-start.2 = (bf16[4,32,264]{2,1,0:T(8,128)(2,1)}, bf16[4,32,264]{2,1,0:T(8,128)(2,1)S(1)}, u32[]{:S(2)}) copy-start(bf16[4,32,264]{2,1,0:T(8,128)(2,1)S(1)} %collective-permute-done.6.left_ref) | copy-start | bytes 202756
  14.5 0.6 copy-start.3
  24.5 55.1 %all-to-all-start.3 = ((bf16[8,2,33,32,128]{4,3,2,1,0:T(8,128)(2,1)}), bf16[8,2,33,32,128]{4,3,2,1,0:T(8,128)(2,1)}, u32[]{:S(2)}, u32[]{:S(2)}) async-start(bf16[8,2,33,32,128]{4,3,2,1,0:T(8,128)(2,1)} %pack0.1), calls=%async_computation.3 | async-start | bytes 8650752 | tf_op jit(solution)/shard_map/all_to_all | solution.py:209
  29.3 6.1 %collective-permute-start.4 = (bf16[4,32,264]{2,1,0:T(8,128)(2,1)S(1)}, bf16[4,32,264]{2,1,0:T(8,128)(2,1)S(1)}, u32[]{:S(2)}, u32[]{:S(2)}) collective-permute-start(bf16[4,32,264]{2,1,0:T(8,128)(2,1)S(1)} %copy.35), channel_id=1, source_target_pairs={{0,8},{8,16},{16,24},{1,9},{9,17},{17,25},{2,10},{10,18},{18,26},{... | collective-permute-start | bytes 202760 | tf_op jit(solution)/shard_map/ppermute | solution.py:190
  33.0 6.7 %collective-permute-start.5 = (bf16[4,32,264]{2,1,0:T(8,128)(2,1)S(1)}, bf16[4,32,264]{2,1,0:T(8,128)(2,1)S(1)}, u32[]{:S(2)}, u32[]{:S(2)}) collective-permute-start(bf16[4,32,264]{2,1,0:T(8,128)(2,1)S(1)} %copy.36), channel_id=1, source_target_pairs={{8,0},{16,8},{24,16},{9,1},{17,9},{25,17},{10,2},{18,10},{26,18},{... | collective-permute-start | bytes 202760 | tf_op jit(solution)/shard_map/ppermute | solution.py:191
  35.4 4.3 %copy-start.5 = (bf16[4,32,264]{2,1,0:T(8,128)(2,1)}, bf16[4,32,264]{2,1,0:T(8,128)(2,1)S(1)}, u32[]{:S(2)}) copy-start(bf16[4,32,264]{2,1,0:T(8,128)(2,1)S(1)} %collective-permute-done.4.left_ref) | copy-start | bytes 202756
  39.6 0.6 copy-start.8
  79.6 55.1 %all-to-all-start.2 = ((bf16[8,2,33,32,128]{4,3,2,1,0:T(8,128)(2,1)}), bf16[8,2,33,32,128]{4,3,2,1,0:T(8,128)(2,1)}, u32[]{:S(2)}, u32[]{:S(2)}) async-start(bf16[8,2,33,32,128]{4,3,2,1,0:T(8,128)(2,1)} %pack1.1), calls=%async_computation.2 | async-start | bytes 8650752 | tf_op jit(solution)/shard_map/all_to_all | solution.py:209
  84.4 6.1 %collective-permute-start.2 = (bf16[4,32,264]{2,1,0:T(8,128)(2,1)S(1)}, bf16[4,32,264]{2,1,0:T(8,128)(2,1)S(1)}, u32[]{:S(2)}, u32[]{:S(2)}) collective-permute-start(bf16[4,32,264]{2,1,0:T(8,128)(2,1)S(1)} %copy.33), channel_id=1, source_target_pairs={{0,8},{8,16},{16,24},{1,9},{9,17},{17,25},{2,10},{10,18},{18,26},{... | collective-permute-start | bytes 202760 | tf_op jit(solution)/shard_map/ppermute | solution.py:190
  88.0 6.7 %collective-permute-start.3 = (bf16[4,32,264]{2,1,0:T(8,128)(2,1)S(1)}, bf16[4,32,264]{2,1,0:T(8,128)(2,1)S(1)}, u32[]{:S(2)}, u32[]{:S(2)}) collective-permute-start(bf16[4,32,264]{2,1,0:T(8,128)(2,1)S(1)} %copy.34), channel_id=1, source_target_pairs={{8,0},{16,8},{24,16},{9,1},{17,9},{25,17},{10,2},{18,10},{26,18},{... | collective-permute-start | bytes 202760 | tf_op jit(solution)/shard_map/ppermute | solution.py:191
  90.5 4.3 %copy-start.6 = (bf16[4,32,264]{2,1,0:T(8,128)(2,1)}, bf16[4,32,264]{2,1,0:T(8,128)(2,1)S(1)}, u32[]{:S(2)}) copy-start(bf16[4,32,264]{2,1,0:T(8,128)(2,1)S(1)} %collective-permute-done.2.left_ref) | copy-start | bytes 202756
  94.7 0.6 copy-start.9
  134.7 55.1 %all-to-all-start.1 = ((bf16[8,2,33,32,128]{4,3,2,1,0:T(8,128)(2,1)}), bf16[8,2,33,32,128]{4,3,2,1,0:T(8,128)(2,1)}, u32[]{:S(2)}, u32[]{:S(2)}) async-start(bf16[8,2,33,32,128]{4,3,2,1,0:T(8,128)(2,1)} %pack2.1), calls=%async_computation.1 | async-start | bytes 8650752 | tf_op jit(solution)/shard_map/all_to_all | solution.py:209
  139.5 6.1 %collective-permute-start = (bf16[4,32,264]{2,1,0:T(8,128)(2,1)S(1)}, bf16[4,32,264]{2,1,0:T(8,128)(2,1)S(1)}, u32[]{:S(2)}, u32[]{:S(2)}) collective-permute-start(bf16[4,32,264]{2,1,0:T(8,128)(2,1)S(1)} %copy.31), channel_id=1, source_target_pairs={{0,8},{8,16},{16,24},{1,9},{9,17},{17,25},{2,10},{10,18},{18,26},{... | collective-permute-start | bytes 202760 | tf_op jit(solution)/shard_map/ppermute | solution.py:190
  143.2 6.7 %collective-permute-start.1 = (bf16[4,32,264]{2,1,0:T(8,128)(2,1)S(1)}, bf16[4,32,264]{2,1,0:T(8,128)(2,1)S(1)}, u32[]{:S(2)}, u32[]{:S(2)}) collective-permute-start(bf16[4,32,264]{2,1,0:T(8,128)(2,1)S(1)} %copy.32), channel_id=1, source_target_pairs={{8,0},{16,8},{24,16},{9,1},{17,9},{25,17},{10,2},{18,10},{26,18},{... | collective-permute-start | bytes 202760 | tf_op jit(solution)/shard_map/ppermute | solution.py:191
  145.6 4.3 %copy-start.4 = (bf16[4,32,264]{2,1,0:T(8,128)(2,1)}, bf16[4,32,264]{2,1,0:T(8,128)(2,1)S(1)}, u32[]{:S(2)}) copy-start(bf16[4,32,264]{2,1,0:T(8,128)(2,1)S(1)} %collective-permute-done.left_ref) | copy-start | bytes 202756
  149.9 0.6 copy-start.7
  159.9 34.6 %copy-start.1 = (s32[16,56,1]{1,2,0:T(1,128)S(1)}, s32[16,56,1]{1,2,0:T(1,128)}, u32[]{:S(2)}) copy-start(s32[16,56,1]{1,2,0:T(1,128)} %param.5) | copy-start | bytes 10756
  189.8 55.1 %all-to-all-start = ((bf16[8,2,33,32,128]{4,3,2,1,0:T(8,128)(2,1)}), bf16[8,2,33,32,128]{4,3,2,1,0:T(8,128)(2,1)}, u32[]{:S(2)}, u32[]{:S(2)}) async-start(bf16[8,2,33,32,128]{4,3,2,1,0:T(8,128)(2,1)} %pack3.1), calls=%async_computation | async-start | bytes 8650752 | tf_op jit(solution)/shard_map/all_to_all | solution.py:209

commit v2 on v1

--- a/solution.py
+++ b/solution.py
@@ -11,14 +11,14 @@
 SHIFT = 32
 LANES = 128
 PAIR = 2
-CHUNKS = 4
 
 
 def turned(values):
     return jnp.transpose(values.astype(jnp.float32))
 
 
-def pack_kernel(base, slots_n, group_ref, order_ref, first_ref, next_ref, wt_ref, left_ref, right_ref, out_ref, rem_ref, w_ref):
+def pack_kernel(base, slots_n, group_ref, order_ref, first_ref, next_ref, wt_ref, left_ref, right_ref, *refs):
+    out_ref, rem_ref, w_ref = refs[-3:]
     step = pl.program_id(0)
     columns, buffer_len = wt_ref.shape[1:]
     full = columns // LANES
@@ -165,8 +165,9 @@
     assert PAIR * slots_n * rem <= LANES and layers % PAIR == 0
     pieces = PAIR * slots_n * full + (1 if rem else 0)
     pairs = layers // PAIR
-    chunks = CHUNKS if pairs % CHUNKS == 0 else 1
-    per = pairs // chunks
+    ends = [max(1, pairs // 4), max(1, pairs // 8)]
+    sizes = [ends[0], pairs - sum(ends), ends[1]] if pairs > sum(ends) else [pairs]
+    firsts = [sum(sizes[:c]) for c in range(len(sizes))]
     width = columns * serve_n
     dtype = train_weights.dtype
 
@@ -180,47 +181,50 @@
     order_in = jnp.sum((same_group & earlier[None]).astype(jnp.int32), axis=2)
     count = jnp.sum((group_ids == serve_idx).astype(jnp.int32), axis=1)
 
-    ends = train_n - 1
-    up = [(i, i + 1) for i in range(ends)]
-    down = [(i + 1, i) for i in range(ends)]
+    up = [(i, i + 1) for i in range(train_n - 1)]
+    down = [(i + 1, i) for i in range(train_n - 1)]
     turned_weights = jnp.swapaxes(train_weights, 1, 2)
-    received = []
-    for c in range(chunks):
-        low, high = c * per * PAIR, (c + 1) * per * PAIR
+
+    def pack(c, after):
+        base, per = firsts[c], sizes[c]
+        low, high = base * PAIR, (base + per) * PAIR
         left = lax.ppermute(train_weights[low:high, buffer_len - SHIFT :], "train", up)
         right = lax.ppermute(train_weights[low:high, :SHIFT], "train", down)
         sent = pl.pallas_call(
-            functools.partial(pack_kernel, c * per, slots_n),
+            functools.partial(pack_kernel, base, slots_n),
             grid_spec=pltpu.PrefetchScalarGridSpec(
                 num_scalar_prefetch=4,
                 grid=(per,),
                 in_specs=[
-                    pl.BlockSpec((PAIR, columns, buffer_len), lambda p, *_, c=c: (c * per + p, 0, 0)),
+                    pl.BlockSpec((PAIR, columns, buffer_len), lambda p, *_: (base + p, 0, 0)),
                     pl.BlockSpec((PAIR, SHIFT, columns), lambda p, *_: (p, 0, 0)),
                     pl.BlockSpec((PAIR, SHIFT, columns), lambda p, *_: (p, 0, 0)),
+                ]
+                + [pl.BlockSpec(memory_space=pl.ANY)] * len(after),
+                out_specs=pl.BlockSpec((serve_n, 1, pieces, BLOCK, LANES), lambda p, *_: (0, p, 0, 0, 0)),
+                scratch_shapes=[
+                    pltpu.VMEM((serve_n, PAIR * slots_n, BLOCK, LANES), dtype),
+                    pltpu.VMEM((PAIR, buffer_len, columns), dtype),
                 ],
-                out_specs=pl.BlockSpec((serve_n, 1, pieces, BLOCK, LANES), lambda p, *_: (0, p, 0, 0, 0)),
-                scratch_shapes=[pltpu.VMEM((serve_n, PAIR * slots_n, BLOCK, LANES), dtype), pltpu.VMEM((PAIR, buffer_len, columns), dtype)],
             ),
             out_shape=jax.ShapeDtypeStruct((serve_n, per, pieces, BLOCK, LANES), dtype),
-            cost_estimate=pl.CostEstimate(flops=0, bytes_accessed=30_000_000 // chunks, transcendentals=0),
+            cost_estimate=pl.CostEstimate(flops=0, bytes_accessed=12_000_000 * per, transcendentals=0),
             name=f"pack{c}",
-        )(group_ids, order_in, first_row, next_row, turned_weights, left, right)
-        received.append(lax.all_to_all(sent, "serve", split_axis=0, concat_axis=0, tiled=True))
-
-    outs = None
-    for c in range(chunks):
-        held = () if outs is None else outs
-        outs = pl.pallas_call(
-            functools.partial(unpack_kernel, c * per, slots_n, columns),
+        )(group_ids, order_in, first_row, next_row, turned_weights, left, right, *after)
+        return lax.all_to_all(sent, "serve", split_axis=0, concat_axis=0, tiled=True)
+
+    def unpack(c, received, held):
+        base, per = firsts[c], sizes[c]
+        return pl.pallas_call(
+            functools.partial(unpack_kernel, base, slots_n, columns),
             grid_spec=pltpu.PrefetchScalarGridSpec(
                 num_scalar_prefetch=1,
                 grid=(per,),
                 in_specs=[pl.BlockSpec((serve_n, 1, pieces, BLOCK, LANES), lambda p, *_: (0, p, 0, 0, 0))]
                 + [pl.BlockSpec(memory_space=pl.ANY)] * len(held),
                 out_specs=[
-                    pl.BlockSpec((PAIR, slots_n, BLOCK, width), lambda p, *_, c=c: (c * per + p, 0, 0, 0)),
-                    pl.BlockSpec((PAIR, slots_n, width), lambda p, *_, c=c: (c * per + p, 0, 0)),
+                    pl.BlockSpec((PAIR, slots_n, BLOCK, width), lambda p, *_: (base + p, 0, 0, 0)),
+                    pl.BlockSpec((PAIR, slots_n, width), lambda p, *_: (base + p, 0, 0)),
                 ],
                 scratch_shapes=[
                     pltpu.VMEM((serve_n, BLOCK, LANES), jnp.float32),
@@ -232,9 +236,18 @@
                 jax.ShapeDtypeStruct((layers, slots_n, width), jnp.float32),
             ],
             input_output_aliases={2: 0, 3: 1} if held else {},
-            cost_estimate=pl.CostEstimate(flops=0, bytes_accessed=40_000_000 // chunks, transcendentals=0),
+            cost_estimate=pl.CostEstimate(flops=0, bytes_accessed=12_000_000 * per, transcendentals=0),
+            compiler_params=pltpu.CompilerParams(vmem_limit_bytes=24 * 1024 * 1024),
             name=f"unpack{c}",
-        )(count, received[c], *held)
+        )(count, received, *held)
+
+    outs, received = (), []
+    for c in range(len(sizes)):
+        if c >= 2:
+            outs = unpack(c - 2, received[c - 2], outs)
+        received.append(pack(c, outs[1:]))
+    for c in range(max(0, len(sizes) - 2), len(sizes)):
+        outs = unpack(c, received[c], outs)
     codes, scales = outs
     return (
         codes.reshape(layers, 1, 1, slots_n, BLOCK, width),

time: 254 us -> 240 us (0.945)
  starting transfers between devices: 39.1 us -> 29.1 us
  Pallas kernels: 69.3 us -> 60.7 us
  waiting for transfers between devices: 135 us -> 138 us
    all_to_all x4 -> x3, waiting for transfers between devices: 116 us -> 127 us  [pack(): lax.all_to_all(sent, 'serve', split_axis=0, concat_axis=0, tiled=True)]
    ppermute x8 -> x6, waiting for transfers between devices: 19.5 us -> 10.5 us  [the longest x3 6.39 us: pack(): right = lax.ppermute(train_weights[low:high, :SHIFT], 'train', down)]
    pallas_call x8 -> x6, Pallas kernels: 69.3 us -> 60.7 us  [the longest x3 33.8 us: pack(): pl.pallas_call(functools.partial(pack_kernel, base, slots_n), grid_spec=p...]
    all_to_all x4 -> x3, starting transfers between devices: 18.5 us -> 13.3 us  [pack(): lax.all_to_all(sent, 'serve', split_axis=0, concat_axis=0, tiled=True)]
    ppermute x8 -> x6, starting transfers between devices: 20.6 us -> 15.8 us  [the longest x3 11.9 us: pack(): lax.ppermute(train_weights[low:high, buffer_len - SHIFT:], 'train', up)]
  transfers between devices with their start and end apart: 12 -> 9, of which waited for: 11 -> 6; matrix products, arithmetic and copies ran while one was open for 1% -> 3% of each run, Pallas kernels for 21% -> 20%
where the time goes in v2:
time: 240 us; the launch traced here: 239 us
  waiting for transfers between devices  138 us (58%)
  Pallas kernels  60.7 us (25%)
  starting transfers between devices  29.1 us (12%)
  local copies, waits for them, and re-layouts  7.11 us (3%)
  other arithmetic  3.38 us (1%)
    all_to_all x3, waiting for transfers between devices, pack(): lax.all_to_all(sent, 'serve', split_axis=0, concat_axis=0, tiled=True)  127 us
    pallas_call x3, Pallas kernels, pack(): pl.pallas_call(functools.partial(pack_kernel, base, slots_n), grid_spec=p...  33.8 us
    pallas_call x3, Pallas kernels, unpack(): pl.pallas_call(functools.partial(unpack_kernel, base, slots_n, columns),...  26.9 us
    all_to_all x3, starting transfers between devices, pack(): lax.all_to_all(sent, 'serve', split_axis=0, concat_axis=0, tiled=True)  13.3 us
    ppermute x3, starting transfers between devices, pack(): lax.ppermute(train_weights[low:high, buffer_len - SHIFT:], 'train', up)  11.9 us
    ppermute x3, waiting for transfers between devices, pack(): right = lax.ppermute(train_weights[low:high, :SHIFT], 'train', down)  6.39 us
  transfers between devices with their start and end apart: 9, of which 6 were waited for; matrix products, arithmetic and copies ran while one was open for 3% of the time, Pallas kernels for 20%

profile of v2, /device:TPU:0, one launch (start us, length us, event | category | flops | bytes accessed | tf_op | source)
XLA Modules:
  0.0 238.9 jit_solution(9624523535399740721)
XLA Ops:
  0.6 1.2 fusion.1
  1.8 0.2 copy.27
  2.0 5.0 %collective-permute-start.2 = (bf16[4,32,264]{2,1,0:T(8,128)(2,1)S(1)}, bf16[4,32,264]{2,1,0:T(8,128)(2,1)S(1)}, u32[]{:S(2)}, u32[]{:S(2)}) collective-permute-start(bf16[4,32,264]{2,1,0:T(8,128)(2,1)S(1)} %copy.27), channel_id=1, source_target_pairs={{0,8},{8,16},{16,24},{1,9},{9,17},{17,25},{2,10},{10,18},{18,26},{... | collective-permute-start | bytes 202760 | tf_op jit(solution)/shard_map/ppermute | solution.py:191
  7.0 0.2 copy.28
  7.1 1.3 collective-permute-start.3
  8.5 0.8 select_reduce_fusion
  9.3 0.6 broadcast_subtract_fusion
  9.9 1.9 convert_reduce_fusion.order_ref
  11.7 0.0 collective-permute-done.2.left_ref
  11.7 1.9 collective-permute-done.3.right_ref
  13.6 0.0 copy-done.3
  13.6 0.6 copy-done.4
  14.3 9.4 %pack0.1 = bf16[8,2,33,32,128]{4,3,2,1,0:T(8,128)(2,1)} custom-call(s32[16,56]{1,0:T(8,128)} %bitcast.14, s32[16,56]{1,0:T(8,128)} %convert_reduce_fusion.order_ref, s32[16]{0:T(128)} %get-tuple-element.27.first_ref, s32[16]{0:T(128)} %get-tuple-element.26.next_ref, bf16[16,264,1856]{2,1,0:T(8,128)(2,1)} %bitcast.8, bf16[4,32,264]{2,1,0:T(8,128)(2,1)} %copy-done.3, ...), custom_call_target="tpu_custom_call" | custom-call | bytes 24000000 | tf_op jit(solution)/shard_map/pack0/pallas_call | solution.py:193
  23.7 4.6 %all-to-all-start = ((bf16[8,2,33,32,128]{4,3,2,1,0:T(8,128)(2,1)}), bf16[8,2,33,32,128]{4,3,2,1,0:T(8,128)(2,1)}, u32[]{:S(2)}, u32[]{:S(2)}) async-start(bf16[8,2,33,32,128]{4,3,2,1,0:T(8,128)(2,1)} %pack0.1), calls=%async_computation | async-start | bytes 8650752 | tf_op jit(solution)/shard_map/all_to_all | solution.py:214
  28.3 1.6 fusion
  29.8 0.4 copy.29
  30.2 3.5 %collective-permute-start.4 = (bf16[10,32,264]{2,1,0:T(8,128)(2,1)S(1)}, bf16[10,32,264]{2,1,0:T(8,128)(2,1)S(1)}, u32[]{:S(2)}, u32[]{:S(2)}) collective-permute-start(bf16[10,32,264]{2,1,0:T(8,128)(2,1)S(1)} %copy.29), channel_id=1, source_target_pairs={{0,8},{8,16},{16,24},{1,9},{9,17},{17,25},{2,10},{10,18},{18,26},{... | collective-permute-start | bytes 506888 | tf_op jit(solution)/shard_map/ppermute | solution.py:191
  33.7 0.3 copy.30
  34.1 1.3 collective-permute-start.5
  35.4 4.1 %collective-permute-done.4.left_ref = bf16[10,32,264]{2,1,0:T(8,128)(2,1)S(1)} collective-permute-done((bf16[10,32,264]{2,1,0:T(8,128)(2,1)S(1)}, bf16[10,32,264]{2,1,0:T(8,128)(2,1)S(1)}, u32[]{:S(2)}, u32[]{:S(2)}) %collective-permute-start.4) | collective-permute-done | bytes 168992 | tf_op jit(solution)/shard_map/ppermute | solution.py:191
  39.4 0.0 copy-start.1
  39.4 4.5 %collective-permute-done.5.right_ref = bf16[10,32,264]{2,1,0:T(8,128)(2,1)S(1)} collective-permute-done((bf16[10,32,264]{2,1,0:T(8,128)(2,1)S(1)}, bf16[10,32,264]{2,1,0:T(8,128)(2,1)S(1)}, u32[]{:S(2)}, u32[]{:S(2)}) %collective-permute-start.5) | collective-permute-done | bytes 168992 | tf_op jit(solution)/shard_map/ppermute | solution.py:192
  43.9 0.0 copy-done.1
  43.9 0.0 copy-start.2
  43.9 0.7 copy-done.2
  44.6 17.8 %pack1.1 = bf16[8,5,33,32,128]{4,3,2,1,0:T(8,128)(2,1)} custom-call(s32[16,56]{1,0:T(8,128)} %bitcast.15, s32[16,56]{1,0:T(8,128)} %convert_reduce_fusion.order_ref, s32[16]{0:T(128)} %get-tuple-element.27.first_ref, s32[16]{0:T(128)} %get-tuple-element.26.next_ref, bf16[16,264,1856]{2,1,0:T(8,128)(2,1)} %bitcast.9, bf16[10,32,264]{2,1,0:T(8,128)(2,1)} %copy-done.1, ...), custom_call_target="tpu_custom_call" | custom-call | bytes 60000000 | tf_op jit(solution)/shard_map/pack1/pallas_call | solution.py:193
  62.4 0.0 copy-start
  62.4 16.4 %all-to-all-done.refs_0_ = bf16[8,2,33,32,128]{4,3,2,1,0:T(8,128)(2,1)} async-done(((bf16[8,2,33,32,128]{4,3,2,1,0:T(8,128)(2,1)}), bf16[8,2,33,32,128]{4,3,2,1,0:T(8,128)(2,1)}, u32[]{:S(2)}, u32[]{:S(2)}) %all-to-all-start) | async-done | bytes 4325408 | tf_op jit(solution)/shard_map/all_to_all | solution.py:214
  78.8 5.2 %all-to-all-start.2 = ((bf16[8,5,33,32,128]{4,3,2,1,0:T(8,128)(2,1)}), bf16[8,5,33,32,128]{4,3,2,1,0:T(8,128)(2,1)}, u32[]{:S(2)}, u32[]{:S(2)}) async-start(bf16[8,5,33,32,128]{4,3,2,1,0:T(8,128)(2,1)} %pack1.1), calls=%async_computation.2 | async-start | bytes 21626880 | tf_op jit(solution)/shard_map/all_to_all | solution.py:214
  83.9 1.1 fusion.2
  85.0 0.1 copy.25
  85.1 3.5 %collective-permute-start = (bf16[2,32,264]{2,1,0:T(8,128)(2,1)S(1)}, bf16[2,32,264]{2,1,0:T(8,128)(2,1)S(1)}, u32[]{:S(2)}, u32[]{:S(2)}) collective-permute-start(bf16[2,32,264]{2,1,0:T(8,128)(2,1)S(1)} %copy.25), channel_id=1, source_target_pairs={{0,8},{8,16},{16,24},{1,9},{9,17},{17,25},{2,10},{10,18},{18,26},{... | collective-permute-start | bytes 101384 | tf_op jit(solution)/shard_map/ppermute | solution.py:191
  88.6 0.1 copy.26
  88.8 1.3 collective-permute-start.1
  90.1 0.0 copy-done
  90.1 0.1 convert_reduce_fusion.1.count_ref
  90.2 7.8 %unpack0.1 = (bf16[16,8,32,2112]{3,2,1,0:T(8,128)(2,1)}, f32[16,8,2112]{2,1,0:T(8,128)}) custom-call(s32[16]{0:T(128)S(1)} %convert_reduce_fusion.1.count_ref, bf16[8,2,33,32,128]{4,3,2,1,0:T(8,128)(2,1)} %all-to-all-done.refs_0_), custom_call_target="tpu_custom_call" | custom-call | bytes 24000000 | tf_op jit(solution)/shard_map/unpack0/pallas_call | solution.py:218
  98.0 0.0 collective-permute-done.left_ref
  98.0 0.0 collective-permute-done.1.right_ref
  98.0 0.0 copy-start.6
  98.1 0.6 copy-done.5
  98.7 0.0 copy-done.6
  98.7 6.6 %pack2.1 = bf16[8,1,33,32,128]{4,3,2,1,0:T(8,128)(2,1)} custom-call(s32[16,56]{1,0:T(8,128)} %bitcast.16, s32[16,56]{1,0:T(8,128)} %convert_reduce_fusion.order_ref, s32[16]{0:T(128)} %get-tuple-element.27.first_ref, s32[16]{0:T(128)} %get-tuple-element.26.next_ref, bf16[16,264,1856]{2,1,0:T(8,128)(2,1)} %bitcast.10, bf16[2,32,264]{2,1,0:T(8,128)(2,1)} %copy-done.5, ...), custom_call_target="tpu_custom_call" | custom-call | bytes 12000000 | tf_op jit(solution)/shard_map/pack2/pallas_call | solution.py:193
  105.3 98.7 %all-to-all-done.2.refs_0_ = bf16[8,5,33,32,128]{4,3,2,1,0:T(8,128)(2,1)} async-done(((bf16[8,5,33,32,128]{4,3,2,1,0:T(8,128)(2,1)}), bf16[8,5,33,32,128]{4,3,2,1,0:T(8,128)(2,1)}, u32[]{:S(2)}, u32[]{:S(2)}) %all-to-all-start.2) | async-done | bytes 10813472 | tf_op jit(solution)/shard_map/all_to_all | solution.py:214
  203.9 3.6 %all-to-all-start.1 = ((bf16[8,1,33,32,128]{4,3,2,1,0:T(8,128)(2,1)}), bf16[8,1,33,32,128]{4,3,2,1,0:T(8,128)(2,1)S(1)}, u32[]{:S(2)}, u32[]{:S(2)}) async-start(bf16[8,1,33,32,128]{4,3,2,1,0:T(8,128)(2,1)} %pack2.1), calls=%async_computation.1 | async-start | bytes 4325376 | tf_op jit(solution)/shard_map/all_to_all | solution.py:214
  207.6 14.9 %unpack1.1 = (bf16[16,8,32,2112]{3,2,1,0:T(8,128)(2,1)}, f32[16,8,2112]{2,1,0:T(8,128)}) custom-call(s32[16]{0:T(128)S(1)} %convert_reduce_fusion.1.count_ref, bf16[8,5,33,32,128]{4,3,2,1,0:T(8,128)(2,1)} %all-to-all-done.2.refs_0_, bf16[16,8,32,2112]{3,2,1,0:T(8,128)(2,1)} %get-tuple-element.9.refs_1_, ...), custom_call_target="tpu_custom_call", output_to_operand_aliasing={{0}: (2, {}), {1}: (3, {})} | custom-call | bytes 60000000 | tf_op jit(solution)/shard_map/unpack1/pallas_call | solution.py:218
  222.5 12.3 %all-to-all-done.1.refs_0_ = bf16[8,1,33,32,128]{4,3,2,1,0:T(8,128)(2,1)S(1)} async-done(((bf16[8,1,33,32,128]{4,3,2,1,0:T(8,128)(2,1)}), bf16[8,1,33,32,128]{4,3,2,1,0:T(8,128)(2,1)S(1)}, u32[]{:S(2)}, u32[]{:S(2)}) %all-to-all-start.1) | async-done | bytes 2162720 | tf_op jit(solution)/shard_map/all_to_all | solution.py:214
  234.8 4.1 %unpack2.1 = (bf16[16,8,32,2112]{3,2,1,0:T(8,128)(2,1)}, f32[16,8,2112]{2,1,0:T(8,128)}) custom-call(s32[16]{0:T(128)S(1)} %convert_reduce_fusion.1.count_ref, bf16[8,1,33,32,128]{4,3,2,1,0:T(8,128)(2,1)S(1)} %all-to-all-done.1.refs_0_, bf16[16,8,32,2112]{3,2,1,0:T(8,128)(2,1)} %get-tuple-element.10.refs_1_, ...), custom_call_target="tpu_custom_call", output_to_operand_aliasing={{0}: (2, {}), {1}: (3, {})} | custom-call | bytes 12000000 | tf_op jit(solution)/shard_map/unpack2/pallas_call | solution.py:218
  (6 shorter events, 0.0 us)
Async XLA Ops:
  2.0 9.7 %collective-permute-start.2 = (bf16[4,32,264]{2,1,0:T(8,128)(2,1)S(1)}, bf16[4,32,264]{2,1,0:T(8,128)(2,1)S(1)}, u32[]{:S(2)}, u32[]{:S(2)}) collective-permute-start(bf16[4,32,264]{2,1,0:T(8,128)(2,1)S(1)} %copy.27), channel_id=1, source_target_pairs={{0,8},{8,16},{16,24},{1,9},{9,17},{17,25},{2,10},{10,18},{18,26},{... | collective-permute-start | bytes 202760 | tf_op jit(solution)/shard_map/ppermute | solution.py:191
  7.1 6.5 %collective-permute-start.3 = (bf16[4,32,264]{2,1,0:T(8,128)(2,1)S(1)}, bf16[4,32,264]{2,1,0:T(8,128)(2,1)S(1)}, u32[]{:S(2)}, u32[]{:S(2)}) collective-permute-start(bf16[4,32,264]{2,1,0:T(8,128)(2,1)S(1)} %copy.28), channel_id=1, source_target_pairs={{8,0},{16,8},{24,16},{9,1},{17,9},{25,17},{10,2},{18,10},{26,18},{... | collective-permute-start | bytes 202760 | tf_op jit(solution)/shard_map/ppermute | solution.py:192
  11.7 1.9 copy-start.3
  13.6 0.6 copy-start.4
  23.7 55.1 %all-to-all-start = ((bf16[8,2,33,32,128]{4,3,2,1,0:T(8,128)(2,1)}), bf16[8,2,33,32,128]{4,3,2,1,0:T(8,128)(2,1)}, u32[]{:S(2)}, u32[]{:S(2)}) async-start(bf16[8,2,33,32,128]{4,3,2,1,0:T(8,128)(2,1)} %pack0.1), calls=%async_computation | async-start | bytes 8650752 | tf_op jit(solution)/shard_map/all_to_all | solution.py:214
  30.2 9.2 %collective-permute-start.4 = (bf16[10,32,264]{2,1,0:T(8,128)(2,1)S(1)}, bf16[10,32,264]{2,1,0:T(8,128)(2,1)S(1)}, u32[]{:S(2)}, u32[]{:S(2)}) collective-permute-start(bf16[10,32,264]{2,1,0:T(8,128)(2,1)S(1)} %copy.29), channel_id=1, source_target_pairs={{0,8},{8,16},{16,24},{1,9},{9,17},{17,25},{2,10},{10,18},{18,26},{... | collective-permute-start | bytes 506888 | tf_op jit(solution)/shard_map/ppermute | solution.py:191
  34.1 9.8 %collective-permute-start.5 = (bf16[10,32,264]{2,1,0:T(8,128)(2,1)S(1)}, bf16[10,32,264]{2,1,0:T(8,128)(2,1)S(1)}, u32[]{:S(2)}, u32[]{:S(2)}) collective-permute-start(bf16[10,32,264]{2,1,0:T(8,128)(2,1)S(1)} %copy.30), channel_id=1, source_target_pairs={{8,0},{16,8},{24,16},{9,1},{17,9},{25,17},{10,2},{18,10},{26,18},{... | collective-permute-start | bytes 506888 | tf_op jit(solution)/shard_map/ppermute | solution.py:192
  39.4 4.5 %copy-start.1 = (bf16[10,32,264]{2,1,0:T(8,128)(2,1)}, bf16[10,32,264]{2,1,0:T(8,128)(2,1)S(1)}, u32[]{:S(2)}) copy-start(bf16[10,32,264]{2,1,0:T(8,128)(2,1)S(1)} %collective-permute-done.4.left_ref) | copy-start | bytes 506884
  43.9 0.7 copy-start.2
  62.4 27.7 %copy-start = (s32[16,56,1]{1,2,0:T(1,128)S(1)}, s32[16,56,1]{1,2,0:T(1,128)}, u32[]{:S(2)}) copy-start(s32[16,56,1]{1,2,0:T(1,128)} %param.5) | copy-start | bytes 10756
  78.8 125.2 %all-to-all-start.2 = ((bf16[8,5,33,32,128]{4,3,2,1,0:T(8,128)(2,1)}), bf16[8,5,33,32,128]{4,3,2,1,0:T(8,128)(2,1)}, u32[]{:S(2)}, u32[]{:S(2)}) async-start(bf16[8,5,33,32,128]{4,3,2,1,0:T(8,128)(2,1)} %pack1.1), calls=%async_computation.2 | async-start | bytes 21626880 | tf_op jit(solution)/shard_map/all_to_all | solution.py:214
  85.1 12.9 %collective-permute-start = (bf16[2,32,264]{2,1,0:T(8,128)(2,1)S(1)}, bf16[2,32,264]{2,1,0:T(8,128)(2,1)S(1)}, u32[]{:S(2)}, u32[]{:S(2)}) collective-permute-start(bf16[2,32,264]{2,1,0:T(8,128)(2,1)S(1)} %copy.25), channel_id=1, source_target_pairs={{0,8},{8,16},{16,24},{1,9},{9,17},{17,25},{2,10},{10,18},{18,26},{... | collective-permute-start | bytes 101384 | tf_op jit(solution)/shard_map/ppermute | solution.py:191
  88.8 9.3 %collective-permute-start.1 = (bf16[2,32,264]{2,1,0:T(8,128)(2,1)S(1)}, bf16[2,32,264]{2,1,0:T(8,128)(2,1)S(1)}, u32[]{:S(2)}, u32[]{:S(2)}) collective-permute-start(bf16[2,32,264]{2,1,0:T(8,128)(2,1)S(1)} %copy.26), channel_id=1, source_target_pairs={{8,0},{16,8},{24,16},{9,1},{17,9},{25,17},{10,2},{18,10},{26,18},{... | collective-permute-start | bytes 101384 | tf_op jit(solution)/shard_map/ppermute | solution.py:192
  98.0 0.6 copy-start.5
  98.0 0.6 copy-start.6
  203.9 30.9 %all-to-all-start.1 = ((bf16[8,1,33,32,128]{4,3,2,1,0:T(8,128)(2,1)}), bf16[8,1,33,32,128]{4,3,2,1,0:T(8,128)(2,1)S(1)}, u32[]{:S(2)}, u32[]{:S(2)}) async-start(bf16[8,1,33,32,128]{4,3,2,1,0:T(8,128)(2,1)} %pack2.1), calls=%async_computation.1 | async-start | bytes 4325376 | tf_op jit(solution)/shard_map/all_to_all | solution.py:214
